TPU v7x, 32 devices: a whole 2x2x4 slice. The times are simulated.
32 devices in a mesh: shard: 8 (over y, x, core), dp: 4 (over z).
Axes of the slice: x: 2, y: 2, z: 4, core: 2. Of those that a mesh axis runs over, the one named last changes fastest.
Arguments:
- grad: float32 [288, 128, 4096], P('shard', 'dp'), may hold values from -252 to 252
- param: bfloat16 [288, 128, 4096], P('shard', 'dp'), may hold values from -0.119628906 to 0.119628906
- row_state: float32 [288, 128], P('shard', 'dp'), may hold values from 0.3 to 27
- col_state: float32 [3, 4096], replicated, may hold values from 0.002 to 400
- block_start: int32 [8], replicated, may hold values from 0 to 143, as said below
- block_matrix: int32 [144], replicated, may hold values from 0 to 2, as said below
- step: int32 [1], replicated, may hold values from 2 to 11
Outputs:
- new_params: bfloat16 [18432, 4096], P(None, 'shard')
- new_row_state: float32 [288, 128], P('shard', 'dp')
- new_col_state: float32 [3, 4096], replicated
Inputs may be any that keep to these rules, and one draw needn't show every extreme that they name: block_start rises from 0 at index 0; every shard index owns between 1 and 36 consecutive global blocks, held in its first slots, and some index owns exactly 36; slots past a device's owned count hold values that no output reads. `block_matrix`: ids 0 and 1 each label 4096 / 128 blocks and id 2 labels 10240 / 128 blocks, in any order.
All inputs are finite; a program needn't handle non-finite values.
Results may differ from a plain program's by a relative error of at most 0.0004.
Values may be sent and summed in bfloat16 or wider, within the bound.
A program may use at most 192 MiB of HBM per device.

v0:
```python
import jax
import jax.numpy as jnp
from jax import lax
from jax.sharding import PartitionSpec as P

D = 4096
FF = 10240


def scale_grad(grad, safe_rows, matrix_pick, new_cols, row_avg):
    slot_cols = jnp.dot(matrix_pick, new_cols, precision=lax.Precision.HIGHEST)
    slot_avg = jnp.dot(matrix_pick, row_avg, precision=lax.Precision.HIGHEST)
    return grad / jnp.sqrt(safe_rows[:, :, None] * slot_cols[:, None, :] / slot_avg[:, None, None])


def body(grad, param, row_state, col_state, block_start, block_matrix, step):
    slot_count = grad.shape[0]
    total_blocks = block_matrix.shape[0]
    shard_index = lax.axis_index("shard")
    block_ends = jnp.concatenate([block_start[1:], jnp.full((1,), total_blocks, jnp.int32)])
    first_block = lax.dynamic_index_in_dim(block_start, shard_index, keepdims=False)
    owned_count = lax.dynamic_index_in_dim(block_ends, shard_index, keepdims=False) - first_block
    slot_ids = jnp.arange(slot_count, dtype=jnp.int32)
    live_slot = slot_ids < owned_count
    block_ids = first_block + slot_ids
    block_table = block_ids[:, None] == jnp.arange(total_blocks, dtype=jnp.int32)[None, :]
    matrix_ids = jnp.sum(jnp.where(block_table, block_matrix[None, :], 0), axis=1)
    matrix_ids = jnp.where(live_slot, matrix_ids, 0)
    matrix_pick = (matrix_ids[:, None] == jnp.arange(3, dtype=jnp.int32)[None, :]).astype(
        jnp.float32
    )
    member = matrix_pick * live_slot[:, None].astype(jnp.float32)
    row_count = jnp.array([D, D, FF], jnp.float32)
    step_value = step[0].astype(jnp.float32)
    decay_rate = 1.0 - step_value ** (-0.8)
    learn_rate = 1.0 / jnp.sqrt(jnp.maximum(step_value, 10000.0))
    squares = grad * grad
    new_rows = jnp.where(
        live_slot[:, None],
        decay_rate * row_state + (1.0 - decay_rate) * jnp.sum(squares, axis=2) / D,
        0.0,
    )
    safe_rows = jnp.where(live_slot[:, None], new_rows, 1.0)
    col_part = jnp.einsum(
        "sm,sd->md", member, jnp.sum(squares, axis=1), precision=lax.Precision.HIGHEST
    )
    row_part = jnp.dot(jnp.sum(new_rows, axis=1), member, precision=lax.Precision.HIGHEST)
    col_total, row_total = lax.psum((col_part, row_part), ("shard", "dp"))
    new_cols = decay_rate * col_state + (1.0 - decay_rate) * col_total / row_count[:, None]
    row_avg = row_total / row_count
    scaled = scale_grad(grad, safe_rows, matrix_pick, new_cols, row_avg)
    square_part = jnp.dot(
        jnp.sum(scaled * scaled, axis=(1, 2)), member, precision=lax.Precision.HIGHEST
    )
    square_total = lax.psum(square_part, ("shard", "dp"))
    clip_factor = jnp.maximum(1.0, jnp.sqrt(square_total / (row_count * D)))
    slot_clip = jnp.dot(matrix_pick, clip_factor, precision=lax.Precision.HIGHEST)
    updated = jnp.where(
        live_slot[:, None, None],
        param.astype(jnp.float32) - learn_rate * scaled / slot_clip[:, None, None],
        0.0,
    ).astype(jnp.bfloat16)
    column_rows = lax.all_to_all(updated, "shard", split_axis=2, concat_axis=0, tiled=True)
    spread = lax.all_gather(column_rows, "dp", axis=1, tiled=True)
    block_index = jnp.arange(total_blocks, dtype=jnp.int32)
    block_owner = (
        jnp.sum((block_start[None, :] <= block_index[:, None]).astype(jnp.int32), axis=1) - 1
    )
    slot_of = block_owner * slot_count + block_index - jnp.take(block_start, block_owner)
    new_params = jnp.take(spread, slot_of, axis=0).reshape(
        total_blocks * spread.shape[1], spread.shape[2]
    )
    return (new_params, new_rows, new_cols)


def solution(mesh):
    return jax.shard_map(
        body,
        mesh=mesh,
        in_specs=(
            P("shard", "dp", None),
            P("shard", "dp", None),
            P("shard", "dp"),
            P(),
            P(),
            P(),
            P(),
        ),
        out_specs=(P(None, "shard"), P("shard", "dp"), P()),
        check_vma=False,
    )
```

profile of v0, /device:TPU:0, one launch (start us, length us, event | category | flops | bytes accessed | tf_op | source)
XLA Modules:
  0.0 1281.9 jit_solution(16187082374226988263)
XLA Ops:
  7.2 0.7 slice.3
  7.9 1.7 fusion.30
  9.7 0.6 dynamic_slice.7
  10.3 0.6 iota_add_fusion
  12.2 0.9 select_reduce_fusion
  13.8 10.8 multiply_reduce_fusion.1
  24.5 0.8 copy.31
  26.4 52.1 %copy.34 = f32[36,32,4096]{0,1,2:T(8,128)} copy(f32[36,32,4096]{2,1,0:T(8,128)} %param.8) | data formatting | bytes 37748736 | tf_op args[0]
  78.5 42.6 %all-reduce = (f32[3]{0:T(128)S(1)}, f32[3,4096]{1,0:T(4,128)S(1)}) all-reduce(f32[3]{0:T(128)S(1)} %convolution_bitcast_fusion.1, f32[3,4096]{1,0:T(4,128)S(1)} %fusion.2), channel_id=1, replica_groups=mesh['shard'=8,'dp'=4] {'shard','dp'}, use_global_device_ids=true, to_apply=%region_6.7 | all-reduce | flops 12291 | bytes 98328 | tf_op jit(solution)/shard_map/psum | solution.py:48
  121.2 1.8 fusion.4
  123.3 21.6 %multiply_reduce_fusion = f32[36]{0:T(128)S(1)} fusion(f32[36,32,4096]{0,1,2:T(8,128)} %copy.34, f32[36]{0:T(128)S(1)} %convolution_bitcast_fusion.3, f32[36,4096]{0,1:T(8,128)S(1)} %fusion.4, f32[36,32]{0,1:T(8,128)S(1)} %copy.32), kind=kLoop, calls=%fused_computation.2 | loop fusion | flops 23592924 | bytes 19469088 | tf_op jit(solution)/shard_map/reduce_sum | solution.py:53
  145.1 40.2 %psum.23 = f32[3]{0:T(128)S(1)} all-reduce(f32[3]{0:T(128)S(1)} %convolution_bitcast_fusion), channel_id=1, replica_groups=mesh['shard'=8,'dp'=4] {'shard','dp'}, use_global_device_ids=true, to_apply=%region_8.9 | all-reduce | flops 3 | bytes 24 | tf_op jit(solution)/shard_map/psum | solution.py:55
  185.4 50.7 %copy.30 = bf16[36,32,4096]{0,1,2:T(8,128)(2,1)} copy(bf16[36,32,4096]{2,1,0:T(8,128)(2,1)} %param.9) | data formatting | bytes 18874368 | tf_op args[1]
  236.2 43.2 %fusion.31 = bf16[4096,32,36]{2,1,0:T(8,128)(2,1)} fusion(f32[36]{0:T(128)S(1)} %convolution_bitcast_fusion.2, f32[36,32,4096]{0,1,2:T(8,128)} %copy.34, f32[36]{0:T(128)S(1)} %convolution_bitcast_fusion.3, f32[36,4096]{0,1:T(8,128)S(1)} %fusion.4, f32[36,32]{0,1:T(8,128)S(1)} %copy.32, f32[]{:T(128)} %bitcast.14, bf16[36,32,4096]{0,1,2:T(8,128)(2,1)} %copy.30, ...), kind=kLoop, calls=%fused_computation.74 | loop fusion | flops 42467328 | bytes 38343496
  279.5 88.9 %reshape.180 = bf16[8,2,294912]{2,1,0:T(2,128)(2,1)} reshape(bf16[4096,32,36]{2,1,0:T(8,128)(2,1)} %fusion.31) | data formatting | bytes 18874368
  368.4 111.2 %all_to_all.18 = bf16[8,2,294912]{2,1,0:T(2,128)(2,1)} all-to-all(bf16[8,2,294912]{2,1,0:T(2,128)(2,1)} %reshape.180), channel_id=1, replica_groups=mesh['shard'=8,'dp'=4] {'shard'}, dimensions={0} | all-to-all | bytes 18874368 | tf_op jit(solution)/shard_map/all_to_all | solution.py:63
  479.6 94.1 %reshape.181 = bf16[4096,32,36]{2,1,0:T(8,128)(2,1)} reshape(bf16[8,2,294912]{2,1,0:T(2,128)(2,1)} %all_to_all.18) | data formatting | bytes 18874368
  573.7 38.9 %copy.36 = bf16[8,36,32,512]{3,2,1,0:T(8,128)(2,1)} copy(bf16[8,36,32,512]{1,2,3,0:T(8,128)(2,1)} %bitcast.51) | data formatting | bytes 18874368 | tf_op jit(solution)/shard_map/all_to_all | solution.py:63
  612.7 0.7 copy.37
  613.5 4.4 compare_select_fusion.2
  617.9 0.6 compare_and_fusion
  618.7 623.5 %all-gather.2.cloned.1.call-done = bf16[288,128,512]{2,1,0:T(8,128)(2,1)} async-done(((bf16[288,32,512]{2,1,0:T(8,128)(2,1)}), bf16[288,128,512]{2,1,0:T(8,128)(2,1)}) %all-gather.2.cloned.1.call-update) | async-done | bytes 37748752 | tf_op jit(solution)/shard_map/all_gather | solution.py:64
  1242.2 15.5 %gather_fusion = bf16[144,128,512]{2,1,0:T(8,128)(2,1)} fusion(bf16[288,128,512]{2,1,0:T(8,128)(2,1)} %all-gather.2.cloned.1.call-done, s32[1024]{0:T(1024)S(1)} %pad_clamp_fusion), kind=kCustom, calls=%fused_computation | custom fusion | bytes 37749312 | tf_op jit(solution)/shard_map/jit(_take)/gather | solution.py:70
  1257.8 17.3 %bitcast_select_fusion = bf16[18432,512]{1,0:T(8,128)(2,1)} fusion(bf16[144,128,512]{2,1,0:T(8,128)(2,1)} %gather_fusion, pred[18432]{0:T(1024)(128)(4,1)S(1)} %broadcast_bitcast_fusion), kind=kLoop, calls=%fused_computation.4 | loop fusion | flops 9437184 | bytes 37767168 | tf_op jit(solution)/shard_map/jit(_take)/select_n | solution.py:70
  (30 shorter events, 2.1 us)
Async XLA Ops:
  7.2 1235.1 %all-gather.2.cloned.1.call-start = ((), (), s32[]{:S(2)}) async-start(), calls=%async_computation.1 | async-start | bytes 47185920 | tf_op jit(solution)/shard_map/all_gather | solution.py:64
  26.4 94.7 %copy-start.1 = (f32[3,4096]{1,0:T(4,128)S(1)}, f32[3,4096]{1,0:T(4,128)}, u32[]{:S(2)}) copy-start(f32[3,4096]{1,0:T(4,128)} %param.11) | copy-start | bytes 147460
  26.4 94.7 %copy-start.3 = (f32[3]{0:T(128)S(1)}, f32[3]{0:T(128)}, u32[]{:S(2)}) copy-start(f32[3]{0:T(128)} %constant.78) | copy-start | bytes 40
  121.2 114.9 %copy-start = (f32[3,4096]{1,0:T(4,128)}, f32[3,4096]{1,0:T(4,128)S(1)}, u32[]{:S(2)}) copy-start(f32[3,4096]{1,0:T(4,128)S(1)} %multiply_add_fusion) | copy-start | bytes 147460
  144.9 91.2 %copy-start.4 = (f32[3]{0:T(128)S(1)}, f32[3]{0:T(128)}, u32[]{:S(2)}) copy-start(f32[3]{0:T(128)} %constant.81) | copy-start | bytes 40
  479.6 133.7 %copy-start.2 = (s32[8]{0:T(128)S(1)}, s32[8]{0:T(128)}, u32[]{:S(2)}) copy-start(s32[8]{0:T(128)} %param.12) | copy-start | bytes 100
Sparse Core Ops, SparseCore 0:
  612.8 629.3 all-gather.1
where the time goes:
time: 1280 us
  waiting for transfers between devices  624 us (49%)
  local copies, waits for them, and re-layouts  345 us (27%)
  blocking collectives  194 us (15%)
  other arithmetic  100 us (8%)
  between operations  16.2 us (1%)
    all_gather x1, waiting for transfers between devices, body(): spread = lax.all_gather(column_rows, 'dp', axis=1, tiled=True)  624 us
    unnamed x16, local copies, waits for them, and re-layouts  287 us
    all_to_all x1, blocking collectives, body(): lax.all_to_all(updated, 'shard', split_axis=2, concat_axis=0, tiled=True)  111 us
    unnamed x1, other arithmetic  43.2 us
    psum x1, blocking collectives, body(): col_total, row_total = lax.psum((col_part, row_part), ('shard', 'dp'))  42.6 us
    psum x1, blocking collectives, body(): square_total = lax.psum(square_part, ('shard', 'dp'))  40.2 us
    all_to_all x1, local copies, waits for them, and re-layouts, body(): lax.all_to_all(updated, 'shard', split_axis=2, concat_axis=0, tiled=True)  38.9 us
  transfers between devices with their start and end apart: 1, of which 1 were waited for; matrix products, arithmetic and copies ran while one was open for 0% of the time, Pallas kernels for 0%

commit v1 on v0

--- a/solution.py
+++ b/solution.py
@@ -60,7 +60,12 @@
         param.astype(jnp.float32) - learn_rate * scaled / slot_clip[:, None, None],
         0.0,
     ).astype(jnp.bfloat16)
-    column_rows = lax.all_to_all(updated, "shard", split_axis=2, concat_axis=0, tiled=True)
+    column_rows = jnp.concatenate(
+        lax.all_to_all(
+            jnp.stack(jnp.split(updated, lax.axis_size("shard"), axis=2)), "shard", 0, 0
+        ),
+        axis=0,
+    )
     spread = lax.all_gather(column_rows, "dp", axis=1, tiled=True)
     block_index = jnp.arange(total_blocks, dtype=jnp.int32)
     block_owner = (

time: 1280 us -> 911 us (0.71)
  local copies, waits for them, and re-layouts: 345 us -> 20.5 us
  other arithmetic: 100 us -> 56 us
    unnamed x16 -> x21, local copies, waits for them, and re-layouts: 287 us -> 1.71 us
    unnamed x1 -> x0, other arithmetic: 43.2 us -> none
    all_to_all x1 -> x0, local copies, waits for them, and re-layouts: 38.9 us -> none  [body(): lax.all_to_all(updated, 'shard', split_axis=2, concat_axis=0, tiled=True)]
    reduce_sum x1, other arithmetic: 21.6 us -> 8.62 us  [body(): jnp.sum(scaled * scaled, axis=(1, 2))]
  transfers between devices with their start and end apart: 1 -> 1, of which waited for: 1 -> 1; matrix products, arithmetic and copies ran while one was open for 0% -> 1% of each run, Pallas kernels for 0% -> 0%
where the time goes in v1:
time: 911 us
  waiting for transfers between devices  624 us (68%)
  blocking collectives  192 us (21%)
  other arithmetic  56 us (6%)
  local copies, waits for them, and re-layouts  20.5 us (2%)
  between operations  16.3 us (2%)
    all_gather x1, waiting for transfers between devices, body(): spread = lax.all_gather(column_rows, 'dp', axis=1, tiled=True)  624 us
    all_to_all x1, blocking collectives, body(): lax.all_to_all(jnp.stack(jnp.split(updated, lax.axis_size('shard'), axis=...  109 us
    psum x1, blocking collectives, body(): col_total, row_total = lax.psum((col_part, row_part), ('shard', 'dp'))  42.6 us
    psum x1, blocking collectives, body(): square_total = lax.psum(square_part, ('shard', 'dp'))  40.1 us
  transfers between devices with their start and end apart: 1, of which 1 were waited for; matrix products, arithmetic and copies ran while one was open for 1% of the time, Pallas kernels for 0%

profile of v1, /device:TPU:0, one launch (start us, length us, event | category | flops | bytes accessed | tf_op | source)
XLA Modules:
  0.0 910.5 jit_solution(1911404698817038510)
XLA Ops:
  7.2 0.7 slice.3
  7.9 1.7 fusion.38
  9.7 0.6 dynamic_slice.7
  10.3 0.6 iota_add_fusion
  12.2 0.9 select_reduce_fusion
  13.8 10.8 %multiply_reduce_fusion.1 = (f32[36,4096]{1,0:T(8,128)S(1)}, f32[36,32]{1,0:T(8,128)S(1)}) fusion(f32[36,32,4096]{2,1,0:T(8,128)} %param.8), kind=kLoop, calls=%fused_computation.5 | loop fusion | flops 14007168 | bytes 19468800 | tf_op jit(solution)/shard_map/reduce_sum | solution.py:45
  24.9 0.6 fusion.10
  25.5 0.2 convolution_bitcast_fusion.1
  25.7 42.6 %all-reduce = (f32[3]{0:T(128)S(1)}, f32[3,4096]{1,0:T(4,128)S(1)}) all-reduce(f32[3]{0:T(128)S(1)} %convolution_bitcast_fusion.1, f32[3,4096]{1,0:T(4,128)S(1)} %fusion.10), channel_id=1, replica_groups=mesh['shard'=8,'dp'=4] {'shard','dp'}, use_global_device_ids=true, to_apply=%region_6.7 | all-reduce | flops 12291 | bytes 98328 | tf_op jit(solution)/shard_map/psum | solution.py:48
  68.4 0.5 fusion.12
  68.9 0.2 convolution_bitcast_fusion.3
  69.1 8.6 multiply_reduce_fusion
  77.7 0.2 convolution_bitcast_fusion
  77.9 40.1 %psum.23 = f32[3]{0:T(128)S(1)} all-reduce(f32[3]{0:T(128)S(1)} %convolution_bitcast_fusion), channel_id=1, replica_groups=mesh['shard'=8,'dp'=4] {'shard','dp'}, use_global_device_ids=true, to_apply=%region_8.9 | all-reduce | flops 3 | bytes 24 | tf_op jit(solution)/shard_map/psum | solution.py:55
  118.0 0.2 convolution_bitcast_fusion.2
  118.2 12.4 %select_convert_fusion = bf16[36,32,4096]{2,1,0:T(8,128)(2,1)S(1)} fusion(bf16[36,32,4096]{2,1,0:T(8,128)(2,1)} %param.9, f32[36]{0:T(128)S(1)} %convolution_bitcast_fusion.2, f32[]{:T(128)} %bitcast.14, pred[36]{0:T(512)(128)(4,1)S(1)} %get-tuple-element.28, f32[36,32,4096]{2,1,0:T(8,128)} %param.8, f32[36]{0:T(128)S(1)} %convolution_bitcast_fusion.3, ...), kind=kLoop, calls=%fused_computation.2 | loop fusion | flops 42467328 | bytes 38343496 | tf_op jit(solution)/shard_map/convert_element_type | solution.py:62
  131.0 0.1 fusion.4
  131.7 109.5 %all_to_all.5 = bf16[8,36,32,512]{3,2,1,0:T(8,128)(2,1)} all-to-all(bf16[8,36,32,512]{3,2,1,0:T(8,128)(2,1)S(1)} %fusion), channel_id=1, replica_groups=mesh['shard'=8,'dp'=4] {'shard'}, dimensions={0} | all-to-all | bytes 18874368 | tf_op jit(solution)/shard_map/all_to_all | solution.py:64
  241.2 0.7 copy.16
  242.0 4.3 compare_select_fusion.2
  246.3 0.7 compare_and_fusion
  247.1 623.8 %all-gather.2.cloned.1.call-done = bf16[288,128,512]{2,1,0:T(8,128)(2,1)} async-done(((bf16[288,32,512]{2,1,0:T(8,128)(2,1)}), bf16[288,128,512]{2,1,0:T(8,128)(2,1)}) %all-gather.2.cloned.1.call-update) | async-done | bytes 37748752 | tf_op jit(solution)/shard_map/all_gather | solution.py:69
  870.8 15.5 %gather_fusion = bf16[144,128,512]{2,1,0:T(8,128)(2,1)} fusion(bf16[288,128,512]{2,1,0:T(8,128)(2,1)} %all-gather.2.cloned.1.call-done, s32[1024]{0:T(1024)S(1)} %pad_clamp_fusion), kind=kCustom, calls=%fused_computation | custom fusion | bytes 37749312 | tf_op jit(solution)/shard_map/jit(_take)/gather | solution.py:75
  886.4 17.3 %bitcast_select_fusion = bf16[18432,512]{1,0:T(8,128)(2,1)} fusion(bf16[144,128,512]{2,1,0:T(8,128)(2,1)} %gather_fusion, pred[18432]{0:T(1024)(128)(4,1)S(1)} %broadcast_bitcast_fusion), kind=kLoop, calls=%fused_computation.1 | loop fusion | flops 9437184 | bytes 37767168 | tf_op jit(solution)/shard_map/jit(_take)/select_n | solution.py:75
  (34 shorter events, 1.7 us)
Async XLA Ops:
  7.2 863.7 %all-gather.2.cloned.1.call-start = ((), (), s32[]{:S(2)}) async-start(), calls=%async_computation.1 | async-start | bytes 47185920 | tf_op jit(solution)/shard_map/all_gather | solution.py:69
  13.8 10.8 %copy-start.3 = (f32[36,32]{0,1:T(8,128)S(1)}, f32[36,32]{0,1:T(8,128)}, u32[]{:S(2)}) copy-start(f32[36,32]{0,1:T(8,128)} %param.10) | copy-start | bytes 13828
  13.8 54.5 %copy-start.1 = (f32[3,4096]{1,0:T(4,128)S(1)}, f32[3,4096]{1,0:T(4,128)}, u32[]{:S(2)}) copy-start(f32[3,4096]{1,0:T(4,128)} %param.11) | copy-start | bytes 147460
  13.8 54.5 %copy-start.4 = (f32[3]{0:T(128)S(1)}, f32[3]{0:T(128)}, u32[]{:S(2)}) copy-start(f32[3]{0:T(128)} %constant.78) | copy-start | bytes 40
  68.4 9.3 %copy-start = (f32[3,4096]{1,0:T(4,128)}, f32[3,4096]{1,0:T(4,128)S(1)}, u32[]{:S(2)}) copy-start(f32[3,4096]{1,0:T(4,128)S(1)} %multiply_add_fusion) | copy-start | bytes 147460
  69.1 48.9 %copy-start.5 = (f32[3]{0:T(128)S(1)}, f32[3]{0:T(128)}, u32[]{:S(2)}) copy-start(f32[3]{0:T(128)} %constant.81) | copy-start | bytes 40
  241.2 0.7 copy-start.2
Sparse Core Ops, SparseCore 0:
  241.3 629.4 all-gather.1
